TPU v7x, 32 devices: a whole 2x2x4 slice. The times are simulated.
32 devices in a mesh: row: 2 (over y), col: 8 (over z, x), rep: 2 (over core).
Axes of the slice: x: 2, y: 2, z: 4, core: 2. Of those that a mesh axis runs over, the one named last changes fastest.
Arguments:
- gain: float32 [48, 8, 128, 128], P(('row', 'col'), 'rep'), as said below
- coupled_columns: int32 [48, 8], P(('row', 'col')), may hold values from 0 to 47, as said below
- solution: float32 [6144, 512], P(('row', 'col')), may hold values from -6 to 6
- residual: float32 [6144, 512], P(('row', 'col')), may hold values from -6 to 6
- direction: float32 [6144, 512], P(('row', 'col')), may hold values from -6 to 6
Outputs:
- solution_next: float32 [6144, 512], P(('row', 'col'))
- residual_next: float32 [6144, 512], P(('row', 'col'))
- direction_next: float32 [6144, 512], P(('row', 'col'))
Inputs may be any that keep to these rules, and one draw needn't show every extreme that they name: `coupled_columns`: each block row i names first its coupled block columns in ascending order (always i - 1, i, i + 1 where inside 0 to 47, some of i - 3, i - 2, i + 2, i + 3, the coupling being symmetric), at most 7 of them, and then fills the remaining slots with i itself; every named column is within 3 of i. The gain matrix assembled from its blocks is symmetric; padding slots hold zero blocks; each diagonal entry exceeds the sum of the absolute values of the other entries of its row by exactly 1.
All inputs are finite; a program needn't handle non-finite values.
Results may differ from a plain program's by a relative error of at most 0.000061.
Values sent between devices are 32-bit elements; how exact they have to be, the bound alone decides.
A program may use at most 64 MiB of HBM per device.

v0:
```python
import jax
import jax.numpy as jnp
from jax import lax
from jax.sharding import PartitionSpec as P

BLK = 128
reach_blocks = 3


def extended_2(block, sides, width):
    for axis, dim in sides:
        count = lax.axis_size(axis)
        forward = [(i, i + 1) for i in range(count - 1)]
        backward = [(target, source) for source, target in forward]
        low = lax.ppermute(
            lax.slice_in_dim(block, block.shape[dim] - width, None, axis=dim), axis, forward
        )
        high = lax.ppermute(lax.slice_in_dim(block, 0, width, axis=dim), axis, backward)
        block = jnp.concatenate([low, block, high], axis=dim)
    return block


def per_device(gain, coupled_columns, solution, residual, direction):
    row_blocks = coupled_columns.shape[0]
    snapshots = direction.shape[1]
    first_block = lax.axis_index(("row", "col")) * row_blocks
    extended = extended_2(direction, ((("row", "col"), 0),), reach_blocks * BLK)
    segments = extended.reshape(row_blocks + 2 * reach_blocks, BLK, snapshots)
    half_slots = gain.shape[1]
    own_columns = lax.dynamic_slice_in_dim(
        coupled_columns, lax.axis_index("rep") * half_slots, half_slots, 1
    )
    local_index = own_columns - first_block + reach_blocks
    picked = segments[local_index]
    product = jnp.einsum(
        "rkab,rkbs->ras",
        gain,
        picked,
        precision=lax.Precision.HIGHEST,
        preferred_element_type=jnp.float32,
    )
    image = lax.psum(product.reshape(row_blocks * BLK, snapshots), "rep")
    norm_old, curvature, crossing, image_square = lax.psum(
        (
            jnp.sum(residual * residual, axis=0),
            jnp.sum(direction * image, axis=0),
            jnp.sum(residual * image, axis=0),
            jnp.sum(image * image, axis=0),
        ),
        ("row", "col"),
    )
    step_size = norm_old / curvature
    solution_next = solution + step_size * direction
    residual_next = residual - step_size * image
    norm_new = norm_old - 2.0 * step_size * crossing + step_size * step_size * image_square
    direction_next = residual_next + norm_new / norm_old * direction
    return (solution_next, residual_next, direction_next)


def solution(mesh):
    return jax.shard_map(
        per_device,
        mesh=mesh,
        in_specs=(
            P(("row", "col"), "rep", None, None),
            P(("row", "col"), None),
            P(("row", "col"), None),
            P(("row", "col"), None),
            P(("row", "col"), None),
        ),
        out_specs=(P(("row", "col"), None), P(("row", "col"), None), P(("row", "col"), None)),
        check_vma=False,
    )
```

profile of v0, /device:TPU:0, one launch (start us, length us, event | category | flops | bytes accessed | tf_op | source)
XLA Modules:
  0.0 132.4 jit_solution(13395826707546090617)
XLA Ops:
  7.2 0.0 copy-start
  7.2 0.0 all-reduce.3.cloned.1.call-start
  7.2 1.4 %collective-permute-start.1 = (f32[384,512]{1,0:T(8,128)}, f32[384,512]{1,0:T(8,128)S(1)}, u32[]{:S(2)}, u32[]{:S(2)}) collective-permute-start(f32[384,512]{1,0:T(8,128)} %param.9), channel_id=1, source_target_pairs={{2,0},{4,2},{6,4},{8,6},{10,8},{12,10},{14,12},{16,14},{18,16},{20... | collective-permute-start | bytes 2359304 | tf_op jit(solution)/shard_map/ppermute | solution.py:18
  8.7 6.4 %collective-permute-start = (f32[384,512]{1,0:T(8,128)}, f32[384,512]{1,0:T(8,128)}, u32[]{:S(2)}, u32[]{:S(2)}) collective-permute-start(f32[384,512]{1,0:T(8,128)} %param.9), channel_id=1, source_target_pairs={{0,2},{2,4},{4,6},{6,8},{8,10},{10,12},{12,14},{14,16},{16,18},{18... | collective-permute-start | bytes 2359304 | tf_op jit(solution)/shard_map/ppermute | solution.py:15
  15.0 0.8 compare_select_fusion
  15.8 0.1 reshape.18
  15.9 30.9 %collective-permute-done.1 = f32[384,512]{1,0:T(8,128)S(1)} collective-permute-done((f32[384,512]{1,0:T(8,128)}, f32[384,512]{1,0:T(8,128)S(1)}, u32[]{:S(2)}, u32[]{:S(2)}) %collective-permute-start.1) | collective-permute-done | bytes 786464 | tf_op jit(solution)/shard_map/ppermute | solution.py:18
  46.8 0.0 copy-start.4
  46.8 0.9 copy-done.4
  47.7 0.0 collective-permute-done
  47.7 1.8 %pad_maximum_fusion = f32[1152,512]{1,0:T(8,128)S(1)} fusion(f32[384,512]{1,0:T(8,128)} %copy-done.4, f32[384,512]{1,0:T(8,128)} %param.9, f32[384,512]{1,0:T(8,128)} %collective-permute-done), kind=kLoop, calls=%fused_computation.1 | loop fusion | flops 1179648 | bytes 4718592 | tf_op jit(solution)/shard_map/concatenate | solution.py:19
  49.5 2.4 %gather_fusion = f32[12,128,512]{2,1,0:T(8,128)} fusion(f32[9,128,512]{2,1,0:T(8,128)S(1)} %bitcast.10, s32[1024]{0:T(1024)S(1)} %pad_clamp_fusion), kind=kCustom, calls=%fused_computation | custom fusion | bytes 6291504 | tf_op jit(solution)/shard_map/gather | solution.py:34
  51.9 0.0 copy-start.1
  51.9 0.0 copy-start.2
  51.9 0.0 copy-done
  52.0 0.0 copy-start.3
  52.0 4.8 %fusion = f32[3,512,128,1]{1,2,3,0:T(8,128)} fusion(f32[3,4,128,512]{3,2,1,0:T(8,128)} %bitcast.11, f32[3,4,128,128]{3,2,1,0:T(8,128)S(1)} %copy-done), kind=kOutput, calls=%fused_computation.12 | convolution fusion | flops 1207959552 | bytes 4718592 | tf_op jit(solution)/shard_map/rkab,rkbs->ras/dot_general | solution.py:35
  56.7 0.0 all-reduce.3.cloned.1.call-update
  56.7 22.1 %all-reduce.3.cloned.1.call-done = f32[384,512]{1,0:T(8,128)} async-done(((f32[384,512]{1,0:T(8,128)}), f32[384,512]{1,0:T(8,128)}) %all-reduce.3.cloned.1.call-update) | async-done | bytes 786448 | tf_op jit(solution)/shard_map/psum | solution.py:42
  78.8 0.0 copy-done.1
  78.8 0.0 copy-done.2
  78.8 1.4 %multiply_reduce_fusion.1 = (f32[512]{0:T(512)S(1)}, f32[512]{0:T(512)S(1)}, f32[512]{0:T(512)S(1)}, f32[512]{0:T(512)S(1)}) fusion(f32[384,512]{1,0:T(8,128)S(1)} %copy-done.2, f32[384,512]{1,0:T(8,128)} %all-reduce.3.cloned.1.call-done, f32[384,512]{1,0:T(8,128)S(1)} %copy-done.1), kind=kLoop, calls=%fused_computation.4 | loop fusion | flops 1570816 | bytes 2367488 | tf_op jit(solution)/shard_map/reduce_sum | solution.py:47
  80.2 42.5 %all-reduce = (f32[512]{0:T(512)S(1)}, f32[512]{0:T(512)S(1)}, f32[512]{0:T(512)S(1)}, f32[512]{0:T(512)S(1)}) all-reduce(f32[512]{0:T(512)S(1)} %get-tuple-element.6, f32[512]{0:T(512)S(1)} %get-tuple-element.5, f32[512]{0:T(512)S(1)} %get-tuple-element.4, ...), channel_id=1, replica_groups=mesh['row'=2,'col'=8,'rep'=2] {'row','col'}, use_global_device_ids=true, to_apply=%region_1.0 | all-reduce | flops 2048 | bytes 16384 | tf_op jit(solution)/shard_map/psum | solution.py:43
  122.8 0.0 copy-done.3
  122.8 2.8 %multiply_add_fusion = (f32[384,512]{1,0:T(8,128)}, f32[384,512]{1,0:T(8,128)}, f32[384,512]{1,0:T(8,128)}) fusion(f32[384,512]{1,0:T(8,128)S(1)} %copy-done.1, f32[512]{0:T(512)S(1)} %get-tuple-element.13, f32[384,512]{1,0:T(8,128)S(1)} %copy-done.2, f32[384,512]{1,0:T(8,128)} %all-reduce.3.cloned.1.call-done, f32[512]{0:T(512)S(1)} %get-tuple-element.14, ...), kind=kLoop, calls=%fused_computation.2 | loop fusion | flops 1179648 | bytes 5509120 | tf_op jit(solution)/shard_map/add | solution.py:56
  (2 shorter events, 0.0 us)
Async XLA Ops:
  7.2 44.8 %copy-start = (f32[3,4,128,128]{3,2,1,0:T(8,128)S(1)}, f32[3,4,128,128]{3,2,1,0:T(8,128)}, u32[]{:S(2)}) copy-start(f32[3,4,128,128]{3,2,1,0:T(8,128)} %param.5) | copy-start | bytes 2359300
  7.2 71.6 %all-reduce.3.cloned.1.call-start = ((), (), s32[]{:S(2)}) async-start(), calls=%async_computation | async-start | bytes 1572864 | tf_op jit(solution)/shard_map/psum | solution.py:42
  7.2 39.6 %collective-permute-start.1 = (f32[384,512]{1,0:T(8,128)}, f32[384,512]{1,0:T(8,128)S(1)}, u32[]{:S(2)}, u32[]{:S(2)}) collective-permute-start(f32[384,512]{1,0:T(8,128)} %param.9), channel_id=1, source_target_pairs={{2,0},{4,2},{6,4},{8,6},{10,8},{12,10},{14,12},{16,14},{18,16},{20... | collective-permute-start | bytes 2359304 | tf_op jit(solution)/shard_map/ppermute | solution.py:18
  8.7 39.1 %collective-permute-start = (f32[384,512]{1,0:T(8,128)}, f32[384,512]{1,0:T(8,128)}, u32[]{:S(2)}, u32[]{:S(2)}) collective-permute-start(f32[384,512]{1,0:T(8,128)} %param.9), channel_id=1, source_target_pairs={{0,2},{2,4},{4,6},{6,8},{8,10},{10,12},{12,14},{14,16},{16,18},{18... | collective-permute-start | bytes 2359304 | tf_op jit(solution)/shard_map/ppermute | solution.py:15
  46.8 0.9 copy-start.4
  51.9 26.9 %copy-start.1 = (f32[384,512]{1,0:T(8,128)S(1)}, f32[384,512]{1,0:T(8,128)}, u32[]{:S(2)}) copy-start(f32[384,512]{1,0:T(8,128)} %param.9) | copy-start | bytes 2359300
  51.9 26.9 %copy-start.2 = (f32[384,512]{1,0:T(8,128)S(1)}, f32[384,512]{1,0:T(8,128)}, u32[]{:S(2)}) copy-start(f32[384,512]{1,0:T(8,128)} %param.8) | copy-start | bytes 2359300
  52.0 70.8 %copy-start.3 = (f32[384,512]{1,0:T(8,128)S(1)}, f32[384,512]{1,0:T(8,128)}, u32[]{:S(2)}) copy-start(f32[384,512]{1,0:T(8,128)} %param.7) | copy-start | bytes 2359300
Sparse Core Ops, SparseCore 0:
  56.9 21.8 all-reduce.2
where the time goes:
time: 133 us; the launch traced here: 132 us
  waiting for transfers between devices  53 us (40%)
  blocking collectives  42.5 us (32%)
  between operations  14.1 us (11%)
  starting transfers between devices  7.85 us (6%)
  other arithmetic  6.84 us (5%)
  matrix products  4.76 us (4%)
  local copies, waits for them, and re-layouts  3.4 us (3%)
    psum x1, blocking collectives, per_device(): lax.psum((jnp.sum(residual * residual, axis=0), jnp.sum(direction * image...  42.5 us
    ppermute x1, waiting for transfers between devices, extended_2(): lax.ppermute(lax.slice_in_dim(block, 0, width, axis=dim), axis, backward)  30.9 us
    psum x1, waiting for transfers between devices, per_device(): image = lax.psum(product.reshape(row_blocks * BLK, snapshots), 'rep')  22.1 us
    ppermute x1, starting transfers between devices, extended_2(): lax.ppermute(lax.slice_in_dim(block, block.shape[dim] - width, None, axis...  6.39 us
    dot_general x1, matrix products, per_device(): jnp.einsum('rkab,rkbs->ras', gain, picked, precision=lax.Precision.HIGHES...  4.76 us
    add x1, other arithmetic, per_device(): direction_next = residual_next + norm_new / norm_old * direction  2.82 us
  transfers between devices with their start and end apart: 3, of which 2 were waited for; matrix products, arithmetic and copies ran while one was open for 1% of the time, Pallas kernels for 0%

commit v1 on v0

--- a/solution.py
+++ b/solution.py
@@ -2,6 +2,7 @@
 import jax.numpy as jnp
 from jax import lax
 from jax.sharding import PartitionSpec as P
+from jax.lax import psum
 
 BLK = 128
 reach_blocks = 3
@@ -40,14 +41,17 @@
         preferred_element_type=jnp.float32,
     )
     image = lax.psum(product.reshape(row_blocks * BLK, snapshots), "rep")
-    norm_old, curvature, crossing, image_square = lax.psum(
-        (
-            jnp.sum(residual * residual, axis=0),
-            jnp.sum(direction * image, axis=0),
-            jnp.sum(residual * image, axis=0),
-            jnp.sum(image * image, axis=0),
+    norm_old, curvature, crossing, image_square = psum(
+        psum(
+            (
+                jnp.sum(residual * residual, axis=0),
+                jnp.sum(direction * image, axis=0),
+                jnp.sum(residual * image, axis=0),
+                jnp.sum(image * image, axis=0),
+            ),
+            axis_name="col",
         ),
-        ("row", "col"),
+        axis_name="row",
     )
     step_size = norm_old / curvature
     solution_next = solution + step_size * direction

time: 133 us -> 117 us (0.88)
  blocking collectives: 42.5 us -> 26.9 us
    psum x1 -> x2, blocking collectives: 42.5 us -> 26.9 us  [the longest x1 21.9 us: per_device(): psum((jnp.sum(residual * residual, axis=0), jnp.sum(direction * image, ax...]
where the time goes in v1:
time: 117 us
  waiting for transfers between devices  53 us (45%)
  blocking collectives  26.9 us (23%)
  between operations  14.1 us (12%)
  starting transfers between devices  7.85 us (7%)
  other arithmetic  6.84 us (6%)
  matrix products  4.76 us (4%)
  local copies, waits for them, and re-layouts  3.4 us (3%)
    ppermute x1, waiting for transfers between devices, extended_2(): lax.ppermute(lax.slice_in_dim(block, 0, width, axis=dim), axis, backward)  30.9 us
    psum x1, waiting for transfers between devices, per_device(): image = lax.psum(product.reshape(row_blocks * BLK, snapshots), 'rep')  22.1 us
    psum x1, blocking collectives, per_device(): psum((jnp.sum(residual * residual, axis=0), jnp.sum(direction * image, ax...  21.9 us
    ppermute x1, starting transfers between devices, extended_2(): lax.ppermute(lax.slice_in_dim(block, block.shape[dim] - width, None, axis...  6.39 us
    psum x1, blocking collectives, per_device(): psum(psum((jnp.sum(residual * residual, axis=0), jnp.sum(direction * imag...  4.99 us
    dot_general x1, matrix products, per_device(): jnp.einsum('rkab,rkbs->ras', gain, picked, precision=lax.Precision.HIGHES...  4.76 us
    add x1, other arithmetic, per_device(): direction_next = residual_next + norm_new / norm_old * direction  2.82 us
    gather x1, local copies, waits for them, and re-layouts, per_device(): picked = segments[local_index]  2.42 us
  transfers between devices with their start and end apart: 3, of which 2 were waited for; matrix products, arithmetic and copies ran while one was open for 1% of the time, Pallas kernels for 0%

profile of v1, /device:TPU:0, one launch (start us, length us, event | category | flops | bytes accessed | tf_op | source)
XLA Modules:
  0.0 116.8 jit_solution(18411321871543987486)
XLA Ops:
  7.2 0.0 copy-start
  7.2 0.0 all-reduce.4.cloned.1.call-start
  7.2 1.4 %collective-permute-start.1 = (f32[384,512]{1,0:T(8,128)}, f32[384,512]{1,0:T(8,128)S(1)}, u32[]{:S(2)}, u32[]{:S(2)}) collective-permute-start(f32[384,512]{1,0:T(8,128)} %param.9), channel_id=1, source_target_pairs={{2,0},{4,2},{6,4},{8,6},{10,8},{12,10},{14,12},{16,14},{18,16},{20... | collective-permute-start | bytes 2359304 | tf_op jit(solution)/shard_map/ppermute | solution.py:19
  8.7 6.4 %collective-permute-start = (f32[384,512]{1,0:T(8,128)}, f32[384,512]{1,0:T(8,128)}, u32[]{:S(2)}, u32[]{:S(2)}) collective-permute-start(f32[384,512]{1,0:T(8,128)} %param.9), channel_id=1, source_target_pairs={{0,2},{2,4},{4,6},{6,8},{8,10},{10,12},{12,14},{14,16},{16,18},{18... | collective-permute-start | bytes 2359304 | tf_op jit(solution)/shard_map/ppermute | solution.py:16
  15.0 0.8 compare_select_fusion
  15.8 0.1 reshape.18
  15.9 30.9 %collective-permute-done.1 = f32[384,512]{1,0:T(8,128)S(1)} collective-permute-done((f32[384,512]{1,0:T(8,128)}, f32[384,512]{1,0:T(8,128)S(1)}, u32[]{:S(2)}, u32[]{:S(2)}) %collective-permute-start.1) | collective-permute-done | bytes 786464 | tf_op jit(solution)/shard_map/ppermute | solution.py:19
  46.8 0.0 copy-start.4
  46.8 0.9 copy-done.4
  47.7 0.0 collective-permute-done
  47.7 1.8 %pad_maximum_fusion = f32[1152,512]{1,0:T(8,128)S(1)} fusion(f32[384,512]{1,0:T(8,128)} %copy-done.4, f32[384,512]{1,0:T(8,128)} %param.9, f32[384,512]{1,0:T(8,128)} %collective-permute-done), kind=kLoop, calls=%fused_computation.1 | loop fusion | flops 1179648 | bytes 4718592 | tf_op jit(solution)/shard_map/concatenate | solution.py:20
  49.5 2.4 %gather_fusion = f32[12,128,512]{2,1,0:T(8,128)} fusion(f32[9,128,512]{2,1,0:T(8,128)S(1)} %bitcast.10, s32[1024]{0:T(1024)S(1)} %pad_clamp_fusion), kind=kCustom, calls=%fused_computation | custom fusion | bytes 6291504 | tf_op jit(solution)/shard_map/gather | solution.py:35
  51.9 0.0 copy-start.1
  51.9 0.0 copy-start.2
  51.9 0.0 copy-done
  52.0 0.0 copy-start.3
  52.0 4.8 %fusion = f32[3,512,128,1]{1,2,3,0:T(8,128)} fusion(f32[3,4,128,512]{3,2,1,0:T(8,128)} %bitcast.11, f32[3,4,128,128]{3,2,1,0:T(8,128)S(1)} %copy-done), kind=kOutput, calls=%fused_computation.12 | convolution fusion | flops 1207959552 | bytes 4718592 | tf_op jit(solution)/shard_map/rkab,rkbs->ras/dot_general | solution.py:36
  56.7 0.0 all-reduce.4.cloned.1.call-update
  56.7 22.1 %all-reduce.4.cloned.1.call-done = f32[384,512]{1,0:T(8,128)} async-done(((f32[384,512]{1,0:T(8,128)}), f32[384,512]{1,0:T(8,128)}) %all-reduce.4.cloned.1.call-update) | async-done | bytes 786448 | tf_op jit(solution)/shard_map/psum | solution.py:43
  78.8 0.0 copy-done.1
  78.8 0.0 copy-done.2
  78.8 1.4 %multiply_reduce_fusion.1 = (f32[512]{0:T(512)S(1)}, f32[512]{0:T(512)S(1)}, f32[512]{0:T(512)S(1)}, f32[512]{0:T(512)S(1)}) fusion(f32[384,512]{1,0:T(8,128)S(1)} %copy-done.2, f32[384,512]{1,0:T(8,128)} %all-reduce.4.cloned.1.call-done, f32[384,512]{1,0:T(8,128)S(1)} %copy-done.1), kind=kLoop, calls=%fused_computation.4 | loop fusion | flops 1570816 | bytes 2367488 | tf_op jit(solution)/shard_map/reduce_sum | solution.py:49
  80.2 21.9 %all-reduce = (f32[512]{0:T(512)S(1)}, f32[512]{0:T(512)S(1)}, f32[512]{0:T(512)S(1)}, f32[512]{0:T(512)S(1)}) all-reduce(f32[512]{0:T(512)S(1)} %get-tuple-element.6, f32[512]{0:T(512)S(1)} %get-tuple-element.5, f32[512]{0:T(512)S(1)} %get-tuple-element.4, f32[512]{0:T(512)S(1)} %get-tuple-element.3), channel_id=1, replica_groups=mesh['row'=2,'col'=8,'rep'=2] {'col'}, use_global_device_ids=true, to_apply=%region_1.0 | all-reduce | flops 2048 | bytes 16384 | tf_op jit(solution)/shard_map/psum | solution.py:45
  102.1 5.0 %all-reduce.1 = (f32[512]{0:T(512)S(1)}, f32[512]{0:T(512)S(1)}, f32[512]{0:T(512)S(1)}, f32[512]{0:T(512)S(1)}) all-reduce(f32[512]{0:T(512)S(1)} %get-tuple-element.7, f32[512]{0:T(512)S(1)} %get-tuple-element.8, f32[512]{0:T(512)S(1)} %get-tuple-element.9, ...), channel_id=1, replica_groups=mesh['row'=2,'col'=8,'rep'=2] {'row'}, use_global_device_ids=true, to_apply=%region_2.0 | all-reduce | flops 2048 | bytes 16384 | tf_op jit(solution)/shard_map/psum | solution.py:44
  107.1 0.0 copy-done.3
  107.1 2.8 %multiply_add_fusion = (f32[384,512]{1,0:T(8,128)}, f32[384,512]{1,0:T(8,128)}, f32[384,512]{1,0:T(8,128)}) fusion(f32[384,512]{1,0:T(8,128)S(1)} %copy-done.1, f32[512]{0:T(512)S(1)} %get-tuple-element.17, f32[384,512]{1,0:T(8,128)S(1)} %copy-done.2, f32[384,512]{1,0:T(8,128)} %all-reduce.4.cloned.1.call-done, f32[512]{0:T(512)S(1)} %get-tuple-element.18, ...), kind=kLoop, calls=%fused_computation.2 | loop fusion | flops 1179648 | bytes 5509120 | tf_op jit(solution)/shard_map/add | solution.py:60
  (2 shorter events, 0.0 us)
Async XLA Ops:
  7.2 44.8 %copy-start = (f32[3,4,128,128]{3,2,1,0:T(8,128)S(1)}, f32[3,4,128,128]{3,2,1,0:T(8,128)}, u32[]{:S(2)}) copy-start(f32[3,4,128,128]{3,2,1,0:T(8,128)} %param.5) | copy-start | bytes 2359300
  7.2 71.6 %all-reduce.4.cloned.1.call-start = ((), (), s32[]{:S(2)}) async-start(), calls=%async_computation | async-start | bytes 1572864 | tf_op jit(solution)/shard_map/psum | solution.py:43
  7.2 39.6 %collective-permute-start.1 = (f32[384,512]{1,0:T(8,128)}, f32[384,512]{1,0:T(8,128)S(1)}, u32[]{:S(2)}, u32[]{:S(2)}) collective-permute-start(f32[384,512]{1,0:T(8,128)} %param.9), channel_id=1, source_target_pairs={{2,0},{4,2},{6,4},{8,6},{10,8},{12,10},{14,12},{16,14},{18,16},{20... | collective-permute-start | bytes 2359304 | tf_op jit(solution)/shard_map/ppermute | solution.py:19
  8.7 39.1 %collective-permute-start = (f32[384,512]{1,0:T(8,128)}, f32[384,512]{1,0:T(8,128)}, u32[]{:S(2)}, u32[]{:S(2)}) collective-permute-start(f32[384,512]{1,0:T(8,128)} %param.9), channel_id=1, source_target_pairs={{0,2},{2,4},{4,6},{6,8},{8,10},{10,12},{12,14},{14,16},{16,18},{18... | collective-permute-start | bytes 2359304 | tf_op jit(solution)/shard_map/ppermute | solution.py:16
  46.8 0.9 copy-start.4
  51.9 26.9 %copy-start.1 = (f32[384,512]{1,0:T(8,128)S(1)}, f32[384,512]{1,0:T(8,128)}, u32[]{:S(2)}) copy-start(f32[384,512]{1,0:T(8,128)} %param.9) | copy-start | bytes 2359300
  51.9 26.9 %copy-start.2 = (f32[384,512]{1,0:T(8,128)S(1)}, f32[384,512]{1,0:T(8,128)}, u32[]{:S(2)}) copy-start(f32[384,512]{1,0:T(8,128)} %param.8) | copy-start | bytes 2359300
  52.0 55.2 %copy-start.3 = (f32[384,512]{1,0:T(8,128)S(1)}, f32[384,512]{1,0:T(8,128)}, u32[]{:S(2)}) copy-start(f32[384,512]{1,0:T(8,128)} %param.7) | copy-start | bytes 2359300
Sparse Core Ops, SparseCore 0:
  56.9 21.8 all-reduce.3
